TPU v7x, 256 devices: a whole 4x4x8 slice. The times are simulated.
256 devices in a mesh: shot: 8 (over y, core), tile: 32 (over x, z).
Axes of the slice: x: 4, y: 4, z: 8, core: 2. Of those that a mesh axis runs over, the one named last changes fastest.
Arguments:
- source: bfloat16 [512, 1, 128, 32, 128], P(('shot', 'tile')), may hold values from -6 to 6
- receiver: bfloat16 [512, 1, 128, 32, 128], P(('shot', 'tile')), may hold values from -6 to 6
- corners: int32 [512, 2], P(('shot', 'tile')), may hold values from 0 to 224, as said below
Outputs:
- filtered: float32 [128, 256, 256], P('tile', 'shot')
Inputs may be any that keep to these rules, and one draw needn't show every extreme that they name: corners[s, 0] is at most 224 and corners[s, 1] at most 128, so every box lies inside the image.
All inputs are finite; a program needn't handle non-finite values.
Results may differ from a plain program's by a relative error of at most 0.0003.
Values may be sent and summed in bfloat16 or wider, within the bound.
A program may use at most 64 MiB of HBM per device.

v0:
```python
import jax
import jax.numpy as jnp
from jax import lax
from jax.sharding import PartitionSpec as P

X = 256
Y = 256


damping = 1.0


def sent_together(arrays, axis, split_dim, concat_dim, along):
    widths = [a.shape[along] for a in arrays]
    both = jnp.concatenate(arrays, axis=along)
    result = lax.all_to_all(both, axis, split_axis=split_dim, concat_axis=concat_dim, tiled=True)
    return tuple(jnp.split(result, [sum(widths[:k]) for k in range(1, len(widths))], axis=along))


def joined_along(parts, dim):
    parts = jnp.moveaxis(parts, 0, dim)
    dims = parts.shape
    return parts.reshape(*dims[:dim], dims[dim] * dims[dim + 1], *dims[dim + 2 :])


def copy_for_each(array, axis):
    copies = jnp.broadcast_to(array, (lax.axis_size(axis), *array.shape))
    return lax.all_to_all(copies, axis, split_axis=0, concat_axis=0, tiled=True)


def gather_directly(array, axis, dim):
    return joined_along(copy_for_each(array, axis), dim)


def split_up(array, dim, length):
    before, after = (array.shape[:dim], array.shape[dim + 1 :])
    return jnp.moveaxis(array.reshape(*before, length, -1, *after), dim, 0)


def sum_at_owner(array, axis, dim):
    parts = split_up(array, dim, lax.axis_size(axis))
    arrived = lax.all_to_all(parts, axis, split_axis=0, concat_axis=0, tiled=True)
    return arrived.sum(axis=0)


def side_by_side(arrays, axis, dim, along):
    widths = [a.shape[along] for a in arrays]
    both = jnp.concatenate(arrays, axis=along)
    result = sum_at_owner(both, axis, dim)
    return tuple(jnp.split(result, [sum(widths[:k]) for k in range(1, len(widths))], axis=along))


def with_halo(array, sides, width):
    edges = {}
    for axis, dim in sides:
        size, length = (lax.axis_size(axis), array.shape[dim])
        up = [(i, (i + 1) % size) for i in range(size - 1)]
        last = lax.slice_in_dim(array, length - width, length, axis=dim)
        initial = lax.slice_in_dim(array, 0, width, axis=dim)
        edges[dim] = (
            lax.ppermute(last, axis, up),
            lax.ppermute(initial, axis, [(b, a) for a, b in up]),
        )
    done = []
    for _, dim in sides:
        low, high = edges[dim]
        around = [(width, width) if d in done else (0, 0) for d in range(array.ndim)]
        array = jnp.concatenate([jnp.pad(low, around), array, jnp.pad(high, around)], axis=dim)
        done.append(dim)
    return array


def laplace(padded):
    center = padded[1:-1, 1:-1, 1:-1]
    beside = padded[2:, 1:-1, 1:-1] + padded[:-2, 1:-1, 1:-1]
    beside = beside + padded[1:-1, 2:, 1:-1] + padded[1:-1, :-2, 1:-1]
    beside = beside + padded[1:-1, 1:-1, 2:] + padded[1:-1, 1:-1, :-2]
    return beside - 6.0 * center


def correlate(wave_bf, back_bf, time_axis):
    wave = wave_bf.astype(jnp.float32)
    back = back_bf.astype(jnp.float32)
    return jnp.stack((jnp.sum(wave * back, axis=time_axis), jnp.sum(wave * wave, axis=time_axis)))


def per_device(source, receiver, corners):
    tile_count = lax.axis_size("tile")
    slab_depth = source.shape[2] // tile_count
    box_rows = source.shape[3]
    box_cols = source.shape[4]
    got_wave, got_back = sent_together((source, receiver), "tile", 2, 0, 1)
    stacked = correlate(got_wave, got_back, 1)
    corner_all = gather_directly(corners, "tile", 0)
    col_index = jnp.arange(Y, dtype=jnp.int32)
    box_col = jnp.arange(box_cols, dtype=jnp.int32)
    col_table = (
        col_index[None, None, :] == corner_all[:, 1][:, None, None] + box_col[None, :, None]
    ).astype(jnp.float32)
    placed = jnp.einsum("qkzab,kby->qzkay", stacked, col_table, precision=lax.Precision.HIGHEST)
    shots_in = corner_all.shape[0]
    placed = placed.reshape(2, slab_depth, shots_in * box_rows, Y)
    row_target = (
        corner_all[:, 0][:, None] + jnp.arange(box_rows, dtype=jnp.int32)[None, :]
    ).reshape(-1)
    row_index = jnp.arange(X, dtype=jnp.int32)
    row_table = (row_target[:, None] == row_index[None, :]).astype(jnp.float32)
    sums = jnp.einsum("rx,qzry->qzxy", row_table, placed, precision=lax.Precision.HIGHEST)
    image_part = sums[0]
    light_part = sums[1]
    image_sum, light_sum = side_by_side((image_part, light_part), "shot", 1, 0)
    normal = image_sum / (damping + light_sum)
    padded = with_halo(normal, (("shot", 1), ("tile", 0)), 1)
    padded = jnp.pad(padded, ((0, 0), (0, 0), (1, 1)))
    return laplace(padded)


def solution(mesh):
    return jax.shard_map(
        per_device,
        mesh=mesh,
        in_specs=(
            P(("shot", "tile"), None, None, None, None),
            P(("shot", "tile"), None, None, None, None),
            P(("shot", "tile"), None),
        ),
        out_specs=P("tile", "shot", None),
        check_vma=False,
    )
```

profile of v0, /device:TPU:1, one launch (start us, length us, event | category | flops | bytes accessed | tf_op | source)
XLA Modules:
  0.0 207.7 jit_solution(12012839073228907743)
XLA Ops:
  0.0 0.8 copy.11
  0.8 0.6 broadcast_in_dim.2
  1.4 11.9 %all-to-all-start = ((s32[32,2,2]{1,2,0:T(2,128)}), s32[32,2,2]{1,2,0:T(2,128)S(1)}, u32[]{:S(2)}, u32[]{:S(2)}) async-start(s32[32,2,2]{1,2,0:T(2,128)} %broadcast_in_dim.2), calls=%async_computation | async-start | bytes 65536 | tf_op jit(solution)/shard_map/all_to_all | solution.py:28
  13.3 2.6 %pad_maximum_fusion = bf16[2,2,128,32,128]{4,3,2,1,0:T(8,128)(2,1)S(1)} fusion(bf16[2,1,128,32,128]{4,3,2,1,0:T(8,128)(2,1)} %param.4, bf16[2,1,128,32,128]{4,3,2,1,0:T(8,128)(2,1)} %param.3), kind=kLoop, calls=%fused_computation.10 | loop fusion | flops 2097152 | bytes 8388608 | tf_op jit(solution)/shard_map/concatenate | solution.py:15
  15.9 3.3 %copy.22 = bf16[2,2,128,32,128]{4,3,1,0,2:T(8,128)(2,1)} copy(bf16[2,2,128,32,128]{4,3,2,1,0:T(8,128)(2,1)S(1)} %pad_maximum_fusion) | data formatting | bytes 8388608 | tf_op jit(solution)/shard_map/concatenate | solution.py:15
  19.2 2.8 %all-to-all-done = s32[32,2,2]{1,2,0:T(2,128)S(1)} async-done(((s32[32,2,2]{1,2,0:T(2,128)}), s32[32,2,2]{1,2,0:T(2,128)S(1)}, u32[]{:S(2)}, u32[]{:S(2)}) %all-to-all-start) | async-done | bytes 544 | tf_op jit(solution)/shard_map/all_to_all | solution.py:28
  22.0 6.5 %all-to-all-start.1 = ((bf16[2,2,128,32,128]{4,3,1,0,2:T(8,128)(2,1)}), bf16[2,2,128,32,128]{4,3,1,0,2:T(8,128)(2,1)}, u32[]{:S(2)}, u32[]{:S(2)}) async-start(bf16[2,2,128,32,128]{4,3,1,0,2:T(8,128)(2,1)} %copy.22), calls=%async_computation.1 | async-start | bytes 8388608 | tf_op jit(solution)/shard_map/all_to_all | solution.py:16
  28.6 0.1 reshape.56
  28.7 0.1 iota_add_fusion
  28.7 0.1 add.74
  28.8 0.1 iota_add_fusion.1
  28.9 94.6 %all-to-all-done.1 = bf16[2,2,128,32,128]{4,3,1,0,2:T(8,128)(2,1)} async-done(((bf16[2,2,128,32,128]{4,3,1,0,2:T(8,128)(2,1)}), bf16[2,2,128,32,128]{4,3,1,0,2:T(8,128)(2,1)}, u32[]{:S(2)}, u32[]{:S(2)}) %all-to-all-start.1) | async-done | bytes 4194336 | tf_op jit(solution)/shard_map/all_to_all | solution.py:16
  123.5 3.5 %copy.15 = bf16[2,2,32,4,32,128]{5,4,3,0,2,1:T(8,128)(2,1)S(1)} copy(bf16[2,2,32,4,32,128]{5,4,1,0,3,2:T(8,128)(2,1)} %bitcast.3) | data formatting | bytes 8388608 | tf_op jit(solution)/shard_map/all_to_all | solution.py:16
  127.0 2.8 %fusion.5 = (f32[1,64,4,32,128]{4,3,2,0,1:T(8,128)S(1)}, f32[1,64,4,32,128]{4,3,2,0,1:T(8,128)}) fusion(bf16[64,2,4,32,128]{4,3,2,0,1:T(8,128)(2,1)S(1)} %bitcast.39), kind=kLoop, calls=%fused_computation.8 | loop fusion | flops 4194304 | bytes 12582912 | tf_op jit(solution)/shard_map/stack | solution.py:84
  129.8 10.3 %convolution_bitcast_fusion = f32[2,4,64,32,256]{4,3,1,0,2:T(8,128)S(1)} fusion(f32[1,64,4,32,128]{4,3,2,0,1:T(8,128)} %get-tuple-element.6, f32[1,64,4,32,128]{4,3,2,0,1:T(8,128)S(1)} %get-tuple-element.5, s32[64,128]{1,0:T(8,128)S(1)} %iota_add_fusion.1), kind=kOutput, calls=%fused_computation | convolution fusion | flops 6446645248 | bytes 25198592 | tf_op jit(solution)/shard_map/qkzab,kby->qzkay/dot_general | solution.py:100
  140.1 6.3 %copy.17 = f32[2,4,64,32,256]{4,3,2,1,0:T(8,128)} copy(f32[2,4,64,32,256]{4,3,1,0,2:T(8,128)S(1)} %convolution_bitcast_fusion) | data formatting | bytes 33554432 | tf_op jit(solution)/shard_map/qkzab,kby->qzkay/transpose | solution.py:100
  146.4 12.1 %fusion.11 = f32[2,4,256,256]{3,2,1,0:T(8,128)S(1)} fusion(f32[2,4,2048,256]{3,2,1,0:T(8,128)} %bitcast.38, s32[2048]{0:T(1024)S(1)} %add.74), kind=kOutput, calls=%fused_computation.17 | convolution fusion | flops 12885426176 | bytes 18882560 | tf_op jit(solution)/shard_map/rx,qzry->qzxy/dot_general | solution.py:108
  158.5 0.1 fusion.22
  158.6 0.2 copy_bitcast_fusion
  158.9 33.5 %all_to_all.28 = f32[8,8,32,256]{3,2,1,0:T(8,128)S(1)} all-to-all(f32[8,8,32,256]{3,2,1,0:T(8,128)S(1)} %copy_bitcast_fusion), channel_id=1, replica_groups=mesh['shot'=8,'tile'=32] {'shot'}, dimensions={0} | all-to-all | bytes 4194304 | tf_op jit(solution)/shard_map/all_to_all | solution.py:42
  192.4 0.2 reduce_sum.8
  192.6 1.3 collective-permute-start.2
  193.9 4.0 %collective-permute-start.3 = (f32[1,32,256]{2,1,0:T(8,128)S(1)}, f32[1,32,256]{2,1,0:T(8,128)S(1)}, u32[]{:S(2)}, u32[]{:S(2)}) collective-permute-start(f32[1,32,256]{2,1,0:T(8,128)S(1)} %get-tuple-element.11), channel_id=1, source_target_pairs={{0,1},{1,2},{2,3},{3,4},{4,5},{5,6},{6,7},{7,8},{8,9},{9,10},{10,1... | collective-permute-start | bytes 98312 | tf_op jit(solution)/shard_map/ppermute | solution.py:61
  197.9 3.9 %collective-permute-start = (f32[4,1,256]{2,1,0:T(1,128)S(1)}, f32[4,1,256]{2,1,0:T(1,128)S(1)}, u32[]{:S(2)}, u32[]{:S(2)}) collective-permute-start(f32[4,1,256]{2,1,0:T(1,128)S(1)} %get-tuple-element.9), channel_id=1, source_target_pairs={{0,32},{32,64},{64,96},{96,128},{128,160},{160,192},{192,224},{1,3... | collective-permute-start | bytes 12296 | tf_op jit(solution)/shard_map/ppermute | solution.py:61
  201.8 1.9 collective-permute-start.1
  203.8 0.0 collective-permute-done.2
  203.8 0.0 collective-permute-done.3
  203.8 0.0 collective-permute-done
  203.8 2.9 %collective-permute-done.1 = f32[4,1,256]{2,1,0:T(1,128)S(1)} collective-permute-done((f32[4,1,256]{2,1,0:T(1,128)S(1)}, f32[4,1,256]{2,1,0:T(1,128)S(1)}, u32[]{:S(2)}, u32[]{:S(2)}) %collective-permute-start.1) | collective-permute-done | bytes 4128 | tf_op jit(solution)/shard_map/ppermute | solution.py:62
  206.8 0.2 select_maximum_fusion
  207.0 0.8 fusion.16
  (7 shorter events, 0.1 us)
Async XLA Ops:
  1.4 20.6 %all-to-all-start = ((s32[32,2,2]{1,2,0:T(2,128)}), s32[32,2,2]{1,2,0:T(2,128)S(1)}, u32[]{:S(2)}, u32[]{:S(2)}) async-start(s32[32,2,2]{1,2,0:T(2,128)} %broadcast_in_dim.2), calls=%async_computation | async-start | bytes 65536 | tf_op jit(solution)/shard_map/all_to_all | solution.py:28
  22.0 101.5 %all-to-all-start.1 = ((bf16[2,2,128,32,128]{4,3,1,0,2:T(8,128)(2,1)}), bf16[2,2,128,32,128]{4,3,1,0,2:T(8,128)(2,1)}, u32[]{:S(2)}, u32[]{:S(2)}) async-start(bf16[2,2,128,32,128]{4,3,1,0,2:T(8,128)(2,1)} %copy.22), calls=%async_computation.1 | async-start | bytes 8388608 | tf_op jit(solution)/shard_map/all_to_all | solution.py:16
  192.6 11.2 %collective-permute-start.2 = (f32[1,32,256]{2,1,0:T(8,128)S(1)}, f32[1,32,256]{2,1,0:T(8,128)S(1)}, u32[]{:S(2)}, u32[]{:S(2)}) collective-permute-start(f32[1,32,256]{2,1,0:T(8,128)S(1)} %get-tuple-element.12), channel_id=1, source_target_pairs={{1,0},{2,1},{3,2},{4,3},{5,4},{6,5},{7,6},{8,7},{9,8},{10,9},{11,1... | collective-permute-start | bytes 98312 | tf_op jit(solution)/shard_map/ppermute | solution.py:62
  193.9 9.9 %collective-permute-start.3 = (f32[1,32,256]{2,1,0:T(8,128)S(1)}, f32[1,32,256]{2,1,0:T(8,128)S(1)}, u32[]{:S(2)}, u32[]{:S(2)}) collective-permute-start(f32[1,32,256]{2,1,0:T(8,128)S(1)} %get-tuple-element.11), channel_id=1, source_target_pairs={{0,1},{1,2},{2,3},{3,4},{4,5},{5,6},{6,7},{7,8},{8,9},{9,10},{10,1... | collective-permute-start | bytes 98312 | tf_op jit(solution)/shard_map/ppermute | solution.py:61
  197.9 5.9 %collective-permute-start = (f32[4,1,256]{2,1,0:T(1,128)S(1)}, f32[4,1,256]{2,1,0:T(1,128)S(1)}, u32[]{:S(2)}, u32[]{:S(2)}) collective-permute-start(f32[4,1,256]{2,1,0:T(1,128)S(1)} %get-tuple-element.9), channel_id=1, source_target_pairs={{0,32},{32,64},{64,96},{96,128},{128,160},{160,192},{192,224},{1,3... | collective-permute-start | bytes 12296 | tf_op jit(solution)/shard_map/ppermute | solution.py:61
  201.8 4.9 %collective-permute-start.1 = (f32[4,1,256]{2,1,0:T(1,128)S(1)}, f32[4,1,256]{2,1,0:T(1,128)S(1)}, u32[]{:S(2)}, u32[]{:S(2)}) collective-permute-start(f32[4,1,256]{2,1,0:T(1,128)S(1)} %get-tuple-element.10), channel_id=1, source_target_pairs={{32,0},{64,32},{96,64},{128,96},{160,128},{192,160},{224,192},{33,... | collective-permute-start | bytes 12296 | tf_op jit(solution)/shard_map/ppermute | solution.py:62
where the time goes:
time: 208 us
  waiting for transfers between devices  100 us (48%)
  blocking collectives  33.5 us (16%)
  starting transfers between devices  29.5 us (14%)
  matrix products  22.4 us (11%)
  local copies, waits for them, and re-layouts  14.8 us (7%)
  other arithmetic  6.95 us (3%)
    all_to_all x1, waiting for transfers between devices, sent_together(): lax.all_to_all(both, axis, split_axis=split_dim, concat_axis=concat_dim,...  94.6 us
    all_to_all x1, blocking collectives, sum_at_owner(): lax.all_to_all(parts, axis, split_axis=0, concat_axis=0, tiled=True)  33.5 us
    dot_general x1, matrix products, per_device(): jnp.einsum('rx,qzry->qzxy', row_table, placed, precision=lax.Precision.HI...  12.1 us
    all_to_all x1, starting transfers between devices, copy_for_each(): return lax.all_to_all(copies, axis, split_axis=0, concat_axis=0, tiled=True)  11.9 us
    dot_general x1, matrix products, per_device(): jnp.einsum('qkzab,kby->qzkay', stacked, col_table, precision=lax.Precisio...  10.3 us
    ppermute x2, starting transfers between devices, with_halo(): lax.ppermute(last, axis, up)  7.9 us
    all_to_all x1, starting transfers between devices, sent_together(): lax.all_to_all(both, axis, split_axis=split_dim, concat_axis=concat_dim,...  6.51 us
    transpose x1, local copies, waits for them, and re-layouts, per_device(): jnp.einsum('qkzab,kby->qzkay', stacked, col_table, precision=lax.Precisio...  6.27 us
  transfers between devices with their start and end apart: 6, of which 3 were waited for; matrix products, arithmetic and copies ran while one was open for 3% of the time, Pallas kernels for 0%

commit v1 on v0

v1 whole, which is shorter than its diff:
```python
import functools

import jax
import jax.numpy as jnp
from jax import lax
from jax.experimental import pallas as pl
from jax.experimental.pallas import tpu as pltpu
from jax.sharding import PartitionSpec as P

MESH = pl.DeviceIdType.MESH
NX, NY, NZ, NC = 4, 4, 8, 2
GROUP = NX * NY * NC
PLANES = NY
X = 256
Y = 256
BX = 32
BY = 128
STRIP = 32
F32 = jnp.float32
BF16 = jnp.bfloat16

ORDER = (
    (1, 0), (0, 1), (3, 3), (2, 1), (0, 3), (1, 2), (3, 0), (2, 2),
    (1, 1), (0, 2), (3, 1), (2, 3), (1, 3), (3, 2), (2, 0), (0, 0),
)


def kernel(
    corners_ref, src_hbm, rcv_hbm, out_ref,
    lbuf, sbuf, rbuf, cmsg, cland, rows, mask, obuf, cbuf, nbuf, fbuf,
    lsem, asend, arecv, csend, crecv, bsend, brecv, nsend, hsend, frecv,
):
    me_w = lax.axis_index("shot")
    me_t = lax.axis_index("tile")
    y, c = me_w // NC, lax.rem(me_w, NC)
    x, z = me_t // NZ, lax.rem(me_t, NZ)
    me_g = x * (NY * NC) + me_w
    up, down = lax.rem(z + 1, NZ), lax.rem(z + NZ - 1, NZ)

    def chip(dx, dy):
        return lax.rem(x + dx, NX), lax.rem(y + dy, NY)

    def remote(src, dst, send, recv, w, t):
        return pltpu.make_async_remote_copy(
            src_ref=src, dst_ref=dst, send_sem=send, recv_sem=recv,
            device_id=(w, t), device_id_type=MESH,
        )

    def depth_of(k):
        half = k // 2
        step = jnp.where(lax.rem(k, 2) == 0, half + 4, 3 - half)
        return lax.rem(z + step, NZ)

    def load(k):
        zt = depth_of(k)
        return (
            pltpu.make_async_copy(src_hbm.at[:, :, zt], lbuf.at[k, 0], lsem.at[k, 0]),
            pltpu.make_async_copy(rcv_hbm.at[:, :, zt], lbuf.at[k, 1], lsem.at[k, 1]),
        )

    @pl.loop(0, NZ)
    def _(k):
        for copy in load(k):
            copy.start()

    barrier = pltpu.get_barrier_semaphore()

    def greet(w, t):
        pl.semaphore_signal(barrier, inc=1, device_id=(w, t), device_id_type=MESH)

    @pl.loop(1, GROUP)
    def _(g):
        other = lax.rem(me_g + g, GROUP)
        greet(lax.rem(other, NY * NC), (other // (NY * NC)) * NZ + z)

    for k in range(NC):
        greet(y * NC + k, x * NZ + up)
        greet(y * NC + k, x * NZ + down)
    last = NX * NZ - 1

    @pl.loop(0, NY * NC)
    def _(w):
        @pl.when(me_t > 0)
        def _():
            greet(w, me_t - 1)

        @pl.when(me_t < last)
        def _():
            greet(w, me_t + 1)

    first_col = [corners_ref[k, 1] for k in range(2)]
    lane = lax.broadcasted_iota(jnp.int32, (1, 128), 1)
    a = lax.rem(lane, BX)
    cmsg[...] = jnp.where(
        lane < 32,
        corners_ref[0, 0] + a,
        jnp.where(
            lane < 64,
            corners_ref[1, 0] + a,
            jnp.where(lane < 96, first_col[0] + 0 * lane, first_col[1] + 0 * lane),
        ),
    )
    cland[me_g] = cmsg[...]
    edges = (me_t > 0).astype(jnp.int32) + (me_t < last).astype(jnp.int32)
    pl.semaphore_wait(barrier, GROUP - 1 + 2 * NC + NY * NC * edges)

    @pl.loop(1, GROUP)
    def _(g):
        other = lax.rem(me_g + g, GROUP)
        remote(
            cmsg, cland.at[me_g], csend, crecv,
            lax.rem(other, NY * NC), (other // (NY * NC)) * NZ + z,
        ).start()

    @pl.loop(0, NZ)
    def _(k):
        for copy in load(k):
            copy.wait()
        for which in range(2):
            for shot in range(2):
                block = lbuf[k, which, shot].reshape(NX * NY * BX, BY).astype(F32)
                block = pltpu.roll(block, lax.rem(first_col[shot], BY), 1).astype(BF16)
                sbuf[pl.ds(k * 16, 16), which, shot] = block.reshape(NX * NY, BX, BY)
        core, q = lax.rem(k, 2), k // 2
        for dx, dy in ORDER:
            tx, ty = chip(dx, dy)

            def send():
                remote(
                    sbuf.at[k * 16 + tx * NY + ty], rbuf.at[q, me_g], asend, arecv.at[q],
                    ty * NC + core, tx * NZ + z,
                ).start()

            if (dx, dy) == (0, 0):
                pl.when(core != c)(send)
            else:
                send()

        @pl.when(core == c)
        def _():
            rbuf[q, me_g] = sbuf[k * 16 + x * NY + y]

    pltpu.make_async_copy(cland.at[pl.ds(0, GROUP - 1)], cland.at[pl.ds(0, GROUP - 1)], crecv).wait()

    @pl.loop(0, GROUP // 4)
    def _(i):
        row = lax.broadcasted_iota(jnp.int32, (X, 128), 0)
        for h in range(2):
            one = cland[4 * i + 2 * h]
            two = cland[4 * i + 2 * h + 1]
            both = jnp.where(lane < 64, one, pltpu.roll(two, 64, 1))
            rows[i, :, pl.ds(h * 128, 128)] = (row == both).astype(F32).astype(BF16)
        wide = lax.broadcasted_iota(jnp.int32, (BX, 128), 1)
        for s in range(4):
            msg = cland[4 * i + s]
            for shot in range(2):
                col = msg[:, 64 + 32 * shot : 65 + 32 * shot]
                left = (wide >= col).astype(F32).astype(BF16)
                mask[i, pl.ds((2 * s + shot) * BX, BX), :] = left

    def place(q):
        pltpu.make_async_copy(
            rbuf.at[q, pl.ds(0, GROUP - 1)], rbuf.at[q, pl.ds(0, GROUP - 1)], arecv.at[q]
        ).wait()

        def step(i, fresh):
            got = rbuf[q, pl.ds(4 * i, 4)]
            wave = got[:, 0].reshape(256, BY).astype(F32)
            back = got[:, 1].reshape(256, BY).astype(F32)
            keep = mask[i]
            table = rows[i]
            for which, value in ((0, wave * back), (1, wave * wave)):
                hi = value.astype(BF16)
                lo = (value - hi.astype(F32)).astype(BF16)
                hi_left, lo_left = hi * keep, lo * keep
                hi_both = jnp.concatenate((hi_left, hi - hi_left), axis=1)
                lo_both = jnp.concatenate((lo_left, lo - lo_left), axis=1)
                part = jnp.dot(table, hi_both, preferred_element_type=F32)
                part = part + jnp.dot(table, lo_both, preferred_element_type=F32)
                if fresh:
                    obuf[q, which] = part
                else:
                    obuf[q, which] += part

        step(0, True)

        @pl.loop(1, GROUP // 4)
        def _(i):
            step(i, False)

    def begin_up():
        return remote(obuf.at[0, 0], cbuf.at[0, 0], bsend.at[0], brecv.at[0], y * NC + 1, x * NZ + up)

    def begin_down():
        return remote(obuf.at[0, 1], cbuf.at[1, 1], bsend.at[1], brecv.at[1], y * NC, x * NZ + down)

    def pass_down(q):
        slot, core = (q + 1, 0) if q < 3 else (4, 1)
        return remote(obuf.at[q], cbuf.at[slot], bsend.at[q + 1], brecv.at[slot], y * NC + core, x * NZ + down)

    def pass_up(q):
        return remote(obuf.at[q], cbuf.at[q + 1], bsend.at[q + 1], brecv.at[q + 1], y * NC + 1, x * NZ + up)

    for q in range(4):
        place(q)

        @pl.when(c == 0)
        def _():
            if q == 0:
                begin_up().start()
                begin_down().start()
            elif q == 1:
                begin_down().wait_recv()
                obuf[1, 1] += cbuf[1, 1]
                pass_down(1).start()
            else:
                pass_down(q - 1).wait_recv()
                obuf[q] += cbuf[q]
                pass_down(q).start()

        @pl.when(c == 1)
        def _():
            if q == 0:
                begin_up().wait_recv()
                obuf[0, 0] += cbuf[0, 0]
                pass_up(0).start()
            elif q < 3:
                pass_up(q - 1).wait_recv()
                obuf[q] += cbuf[q]
                pass_up(q).start()
            else:
                pass_up(2).wait_recv()
                pass_down(3).wait_recv()

    def to_strip(w):
        return remote(
            nbuf.at[pl.ds(pl.multiple_of(w * STRIP, 8), STRIP + 16)], fbuf.at[1 + y],
            nsend.at[w], frecv.at[1 + y], w, me_t,
        )

    def to_side(w, plane, t):
        return remote(
            nbuf.at[pl.ds(pl.multiple_of(w * STRIP + 8, 8), STRIP)], fbuf.at[plane, pl.ds(8, STRIP)],
            hsend.at[w], frecv.at[plane], w, t,
        )

    to_later = jnp.logical_and(y == NY - 1, me_t < last)
    to_earlier = jnp.logical_and(y == 0, me_t > 0)

    @pl.when(c == 1)
    def _():
        image = obuf[3, 0] + cbuf[3, 0] + cbuf[4, 0]
        light = obuf[3, 1] + cbuf[3, 1] + cbuf[4, 1]
        nbuf[pl.ds(0, 8)] = jnp.zeros((8, Y), F32)
        nbuf[pl.ds(X + 8, 8)] = jnp.zeros((8, Y), F32)
        nbuf[pl.ds(8, X)] = image / (1.0 + light)

        @pl.loop(1, NY * NC)
        def _(k):
            to_strip(lax.rem(me_w + k, NY * NC)).start()

        @pl.loop(0, NY * NC)
        def _(k):
            w = lax.rem(me_w + k, NY * NC)

            @pl.when(to_later)
            def _():
                to_side(w, 0, me_t + 1).start()

            @pl.when(to_earlier)
            def _():
                to_side(w, 5, me_t - 1).start()

        fbuf[1 + y] = nbuf[pl.ds(pl.multiple_of(me_w * STRIP, 8), STRIP + 16)]

    @pl.when(me_t == 0)
    def _():
        fbuf[0] = jnp.zeros((STRIP + 16, Y), F32)

    @pl.when(me_t == last)
    def _():
        fbuf[5] = jnp.zeros((STRIP + 16, Y), F32)

    for j in range(PLANES):

        @pl.when(jnp.logical_not(jnp.logical_and(c == 1, y == j)))
        def _():
            pltpu.make_async_copy(fbuf.at[1 + j], fbuf.at[1 + j], frecv.at[1 + j]).wait()

    @pl.when(me_t > 0)
    def _():
        pltpu.make_async_copy(fbuf.at[0, pl.ds(8, STRIP)], fbuf.at[0, pl.ds(8, STRIP)], frecv.at[0]).wait()

    @pl.when(me_t < last)
    def _():
        pltpu.make_async_copy(fbuf.at[5, pl.ds(8, STRIP)], fbuf.at[5, pl.ds(8, STRIP)], frecv.at[5]).wait()

    column = lax.broadcasted_iota(jnp.int32, (STRIP, Y), 1)
    for j in range(PLANES):
        center = fbuf[1 + j, pl.ds(8, STRIP)]
        beside = fbuf[j, pl.ds(8, STRIP)] + fbuf[2 + j, pl.ds(8, STRIP)]
        beside = beside + fbuf[1 + j, pl.ds(7, STRIP)] + fbuf[1 + j, pl.ds(9, STRIP)]
        before = jnp.where(column == 0, 0.0, pltpu.roll(center, 1, 1))
        after = jnp.where(column == Y - 1, 0.0, pltpu.roll(center, Y - 1, 1))
        out_ref[j] = beside + (before + after) - 6.0 * center

    pltpu.make_async_copy(sbuf.at[pl.ds(0, 124)], sbuf.at[pl.ds(0, 124)], asend).wait()
    pltpu.make_async_copy(cland.at[pl.ds(0, GROUP - 1)], cland.at[pl.ds(0, GROUP - 1)], csend).wait()

    @pl.when(c == 0)
    def _():
        begin_up().wait_send()
        begin_down().wait_send()
        for q in range(1, 4):
            pass_down(q).wait_send()

    @pl.when(c == 1)
    def _():
        for q in range(3):
            pass_up(q).wait_send()

        @pl.loop(1, NY * NC)
        def _(k):
            to_strip(lax.rem(me_w + k, NY * NC)).wait_send()

        @pl.loop(0, NY * NC)
        def _(k):
            w = lax.rem(me_w + k, NY * NC)

            @pl.when(to_later)
            def _():
                to_side(w, 0, me_t + 1).wait_send()

            @pl.when(to_earlier)
            def _():
                to_side(w, 5, me_t - 1).wait_send()


def per_device(source, receiver, corners):
    source = source.reshape(2, NX, NZ, PLANES, BX, BY)
    receiver = receiver.reshape(2, NX, NZ, PLANES, BX, BY)
    dma = pltpu.SemaphoreType.DMA
    return pl.pallas_call(
        kernel,
        out_shape=jax.ShapeDtypeStruct((PLANES, STRIP, Y), F32),
        in_specs=[
            pl.BlockSpec(memory_space=pltpu.SMEM),
            pl.BlockSpec(memory_space=pl.ANY),
            pl.BlockSpec(memory_space=pl.ANY),
        ],
        out_specs=pl.BlockSpec(memory_space=pltpu.VMEM),
        scratch_shapes=[
            pltpu.VMEM((NZ, 2, 2, NX, NY, BX, BY), BF16),
            pltpu.VMEM((NZ * NX * NY, 2, 2, BX, BY), BF16),
            pltpu.VMEM((4, GROUP, 2, 2, BX, BY), BF16),
            pltpu.VMEM((1, 128), jnp.int32),
            pltpu.VMEM((GROUP, 1, 128), jnp.int32),
            pltpu.VMEM((GROUP // 4, X, 256), BF16),
            pltpu.VMEM((GROUP // 4, 256, 128), BF16),
            pltpu.VMEM((4, 2, X, Y), F32),
            pltpu.VMEM((5, 2, X, Y), F32),
            pltpu.VMEM((X + 16, Y), F32),
            pltpu.VMEM((PLANES + 2, STRIP + 16, Y), F32),
            dma((NZ, 2)), dma, dma((4,)), dma, dma,
            dma((5,)), dma((5,)), dma((8,)), dma((8,)), dma((6,)),
        ],
        compiler_params=pltpu.CompilerParams(
            collective_id=0, has_side_effects=True, vmem_limit_bytes=48 << 20
        ),
        name="stack_shots",
    )(corners, source, receiver)


def solution(mesh):
    return jax.shard_map(
        per_device,
        mesh=mesh,
        in_specs=(
            P(("shot", "tile"), None, None, None, None),
            P(("shot", "tile"), None, None, None, None),
            P(("shot", "tile"), None),
        ),
        out_specs=P("tile", "shot", None),
        check_vma=False,
    )
```

time: 208 us -> 77.1 us (0.37)
  the two profiles are of different devices: /device:TPU:1 before, /device:TPU:3 now
where the time goes in v1:
time: 77.1 us; the launch traced here: 77 us
  Pallas kernels  72.4 us (94%)
  local copies, waits for them, and re-layouts  4.52 us (6%)
    pallas_call x1, Pallas kernels, per_device(): pl.pallas_call(kernel, out_shape=jax.ShapeDtypeStruct((PLANES, STRIP, Y),...  72.4 us
    unnamed x7, local copies, waits for them, and re-layouts  4.52 us

profile of v1, /device:TPU:3, one launch (start us, length us, event | category | flops | bytes accessed | tf_op | source)
XLA Modules:
  0.0 77.0 jit_solution(7911459793708769497)
XLA Ops:
  0.0 0.0 copy-start
  0.0 1.6 %copy-done = bf16[2,1,128,32,128]{4,3,2,1,0:T(8,128)(2,1)S(1)} copy-done((bf16[2,1,128,32,128]{4,3,2,1,0:T(8,128)(2,1)S(1)}, bf16[2,1,128,32,128]{4,3,2,1,0:T(8,128)(2,1)}, u32[]{:S(2)}) %copy-start) | copy-done | bytes 2097176
  1.6 0.0 copy-start.1
  1.6 1.6 %copy-done.1 = bf16[2,1,128,32,128]{4,3,2,1,0:T(8,128)(2,1)S(1)} copy-done((bf16[2,1,128,32,128]{4,3,2,1,0:T(8,128)(2,1)S(1)}, bf16[2,1,128,32,128]{4,3,2,1,0:T(8,128)(2,1)}, u32[]{:S(2)}) %copy-start.1) | copy-done | bytes 2097176
  3.2 0.0 copy-start.2
  3.2 0.7 copy-done.2
  3.9 72.4 %stack_shots.1 = f32[4,32,256]{2,1,0:T(8,128)S(1)} custom-call(s32[2,2]{1,0:T(2,128)S(1)} %copy-done.2, bf16[2,4,8,4,32,128]{5,4,3,2,1,0:T(8,128)(2,1)S(1)} %bitcast.2, bf16[2,4,8,4,32,128]{5,4,3,2,1,0:T(8,128)(2,1)S(1)} %bitcast.3), custom_call_target="tpu_custom_call" | custom-call | tf_op jit(solution)/shard_map/stack_shots/pallas_call | solution.py:343
  76.3 0.7 copy.5
Async XLA Ops:
  0.0 1.6 %copy-start = (bf16[2,1,128,32,128]{4,3,2,1,0:T(8,128)(2,1)S(1)}, bf16[2,1,128,32,128]{4,3,2,1,0:T(8,128)(2,1)}, u32[]{:S(2)}) copy-start(bf16[2,1,128,32,128]{4,3,2,1,0:T(8,128)(2,1)} %param.3) | copy-start | bytes 6291460
  1.6 1.6 %copy-start.1 = (bf16[2,1,128,32,128]{4,3,2,1,0:T(8,128)(2,1)S(1)}, bf16[2,1,128,32,128]{4,3,2,1,0:T(8,128)(2,1)}, u32[]{:S(2)}) copy-start(bf16[2,1,128,32,128]{4,3,2,1,0:T(8,128)(2,1)} %param.4) | copy-start | bytes 6291460
  3.2 0.7 copy-start.2

commit v2 on v1

--- a/solution.py
+++ b/solution.py
@@ -26,9 +26,9 @@
 
 
 def kernel(
-    corners_ref, src_hbm, rcv_hbm, out_ref,
-    lbuf, sbuf, rbuf, cmsg, cland, rows, mask, obuf, cbuf, nbuf, fbuf,
-    lsem, asend, arecv, csend, crecv, bsend, brecv, nsend, hsend, frecv,
+    corners_hbm, src_hbm, rcv_hbm, out_ref,
+    corners_ref, lbuf, sbuf, rbuf, cmsg, cland, rows, mask, obuf, cbuf, nbuf, fbuf,
+    cornersem, lsem, asend, arecv, csend, crecv, bsend, brecv, nsend, hsend, frecv,
 ):
     me_w = lax.axis_index("shot")
     me_t = lax.axis_index("tile")
@@ -58,6 +58,9 @@
             pltpu.make_async_copy(rcv_hbm.at[:, :, zt], lbuf.at[k, 1], lsem.at[k, 1]),
         )
 
+    corners_copy = pltpu.make_async_copy(corners_hbm, corners_ref, cornersem)
+    corners_copy.start()
+
     @pl.loop(0, NZ)
     def _(k):
         for copy in load(k):
@@ -88,6 +91,7 @@
         def _():
             greet(w, me_t + 1)
 
+    corners_copy.wait()
     first_col = [corners_ref[k, 1] for k in range(2)]
     lane = lax.broadcasted_iota(jnp.int32, (1, 128), 1)
     a = lax.rem(lane, BX)
@@ -344,12 +348,13 @@
         kernel,
         out_shape=jax.ShapeDtypeStruct((PLANES, STRIP, Y), F32),
         in_specs=[
-            pl.BlockSpec(memory_space=pltpu.SMEM),
-            pl.BlockSpec(memory_space=pl.ANY),
-            pl.BlockSpec(memory_space=pl.ANY),
+            pl.BlockSpec(memory_space=pltpu.HBM),
+            pl.BlockSpec(memory_space=pltpu.HBM),
+            pl.BlockSpec(memory_space=pltpu.HBM),
         ],
         out_specs=pl.BlockSpec(memory_space=pltpu.VMEM),
         scratch_shapes=[
+            pltpu.SMEM((2, 2), jnp.int32),
             pltpu.VMEM((NZ, 2, 2, NX, NY, BX, BY), BF16),
             pltpu.VMEM((NZ * NX * NY, 2, 2, BX, BY), BF16),
             pltpu.VMEM((4, GROUP, 2, 2, BX, BY), BF16),
@@ -361,11 +366,11 @@
             pltpu.VMEM((5, 2, X, Y), F32),
             pltpu.VMEM((X + 16, Y), F32),
             pltpu.VMEM((PLANES + 2, STRIP + 16, Y), F32),
-            dma((NZ, 2)), dma, dma((4,)), dma, dma,
+            dma, dma((NZ, 2)), dma, dma((4,)), dma, dma,
             dma((5,)), dma((5,)), dma((8,)), dma((8,)), dma((6,)),
         ],
         compiler_params=pltpu.CompilerParams(
-            collective_id=0, has_side_effects=True, vmem_limit_bytes=48 << 20
+            collective_id=0, has_side_effects=True, vmem_limit_bytes=67043328
         ),
         name="stack_shots",
     )(corners, source, receiver)

time: 77.1 us -> 73.8 us (0.957)
  local copies, waits for them, and re-layouts: 4.52 us -> 1.57 us
    unnamed x7 -> x1, local copies, waits for them, and re-layouts: 4.52 us -> 1.57 us
where the time goes in v2:
time: 73.8 us; the launch traced here: 73.7 us
  Pallas kernels  72.2 us (98%)
  local copies, waits for them, and re-layouts  1.57 us (2%)
    pallas_call x1, Pallas kernels, per_device(): pl.pallas_call(kernel, out_shape=jax.ShapeDtypeStruct((PLANES, STRIP, Y),...  72.2 us
    unnamed x1, local copies, waits for them, and re-layouts  1.57 us

profile of v2, /device:TPU:3, one launch (start us, length us, event | category | flops | bytes accessed | tf_op | source)
XLA Modules:
  0.0 73.7 jit_solution(9897450493529739280)
XLA Ops:
  0.0 72.2 %stack_shots.1 = f32[4,32,256]{2,1,0:T(8,128)} custom-call(s32[2,2]{1,0:T(2,128)} %corners_hbm.1, bf16[2,4,8,4,32,128]{5,4,3,2,1,0:T(8,128)(2,1)} %bitcast.2, bf16[2,4,8,4,32,128]{5,4,3,2,1,0:T(8,128)(2,1)} %bitcast.3), custom_call_target="tpu_custom_call" | custom-call | tf_op jit(solution)/shard_map/stack_shots/pallas_call | solution.py:347
  72.2 1.6 %copy.5 = f32[4,32,256]{2,1,0:T(8,128)} copy(f32[4,32,256]{2,1,0:T(8,128)} %stack_shots.1) | data formatting | bytes 262144

commit v3 on v2

--- a/solution.py
+++ b/solution.py
@@ -10,6 +10,7 @@
 MESH = pl.DeviceIdType.MESH
 NX, NY, NZ, NC = 4, 4, 8, 2
 GROUP = NX * NY * NC
+BLOCKS = GROUP // 4
 PLANES = NY
 X = 256
 Y = 256
@@ -27,14 +28,15 @@
 
 def kernel(
     corners_hbm, src_hbm, rcv_hbm, out_ref,
-    corners_ref, lbuf, sbuf, rbuf, cmsg, cland, rows, mask, obuf, cbuf, nbuf, fbuf,
-    cornersem, lsem, asend, arecv, csend, crecv, bsend, brecv, nsend, hsend, frecv,
+    corners_ref, lbuf, head_out, sbuf, head_in, rbuf, rows, mask, obuf, cbuf, nbuf, fbuf,
+    cornersem, lsem, headsend, asend, arecv, bsend, brecv, nsend, hsend, frecv,
 ):
     me_w = lax.axis_index("shot")
     me_t = lax.axis_index("tile")
     y, c = me_w // NC, lax.rem(me_w, NC)
     x, z = me_t // NZ, lax.rem(me_t, NZ)
     me_g = x * (NY * NC) + me_w
+    me_slot = 2 * (NX * NY - 1) + c
     up, down = lax.rem(z + 1, NZ), lax.rem(z + NZ - 1, NZ)
 
     def chip(dx, dy):
@@ -58,6 +60,31 @@
             pltpu.make_async_copy(rcv_hbm.at[:, :, zt], lbuf.at[k, 1], lsem.at[k, 1]),
         )
 
+    barrier = pltpu.get_barrier_semaphore()
+
+    def greet(w, t):
+        pl.semaphore_signal(barrier, inc=1, device_id=(w, t), device_id_type=MESH)
+
+    @pl.loop(1, GROUP)
+    def _(g):
+        other = lax.rem(me_g + g, GROUP)
+        greet(lax.rem(other, NY * NC), (other // (NY * NC)) * NZ + z)
+
+    for k in range(NC):
+        greet(y * NC + k, x * NZ + up)
+        greet(y * NC + k, x * NZ + down)
+    last = NX * NZ - 1
+
+    @pl.loop(0, NY * NC)
+    def _(w):
+        @pl.when(me_t > 0)
+        def _():
+            greet(w, me_t - 1)
+
+        @pl.when(me_t < last)
+        def _():
+            greet(w, me_t + 1)
+
     corners_copy = pltpu.make_async_copy(corners_hbm, corners_ref, cornersem)
     corners_copy.start()
 
@@ -66,36 +93,11 @@
         for copy in load(k):
             copy.start()
 
-    barrier = pltpu.get_barrier_semaphore()
-
-    def greet(w, t):
-        pl.semaphore_signal(barrier, inc=1, device_id=(w, t), device_id_type=MESH)
-
-    @pl.loop(1, GROUP)
-    def _(g):
-        other = lax.rem(me_g + g, GROUP)
-        greet(lax.rem(other, NY * NC), (other // (NY * NC)) * NZ + z)
-
-    for k in range(NC):
-        greet(y * NC + k, x * NZ + up)
-        greet(y * NC + k, x * NZ + down)
-    last = NX * NZ - 1
-
-    @pl.loop(0, NY * NC)
-    def _(w):
-        @pl.when(me_t > 0)
-        def _():
-            greet(w, me_t - 1)
-
-        @pl.when(me_t < last)
-        def _():
-            greet(w, me_t + 1)
-
     corners_copy.wait()
     first_col = [corners_ref[k, 1] for k in range(2)]
-    lane = lax.broadcasted_iota(jnp.int32, (1, 128), 1)
+    lane = lax.broadcasted_iota(jnp.int32, (8, 128), 1)
     a = lax.rem(lane, BX)
-    cmsg[...] = jnp.where(
+    note = jnp.where(
         lane < 32,
         corners_ref[0, 0] + a,
         jnp.where(
@@ -104,73 +106,90 @@
             jnp.where(lane < 96, first_col[0] + 0 * lane, first_col[1] + 0 * lane),
         ),
     )
-    cland[me_g] = cmsg[...]
-    edges = (me_t > 0).astype(jnp.int32) + (me_t < last).astype(jnp.int32)
-    pl.semaphore_wait(barrier, GROUP - 1 + 2 * NC + NY * NC * edges)
-
-    @pl.loop(1, GROUP)
-    def _(g):
-        other = lax.rem(me_g + g, GROUP)
-        remote(
-            cmsg, cland.at[me_g], csend, crecv,
-            lax.rem(other, NY * NC), (other // (NY * NC)) * NZ + z,
-        ).start()
-
-    @pl.loop(0, NZ)
-    def _(k):
+    note = note.astype(F32).astype(BF16)
+
+    def turn(k, out, at):
         for copy in load(k):
             copy.wait()
         for which in range(2):
             for shot in range(2):
                 block = lbuf[k, which, shot].reshape(NX * NY * BX, BY).astype(F32)
                 block = pltpu.roll(block, lax.rem(first_col[shot], BY), 1).astype(BF16)
-                sbuf[pl.ds(k * 16, 16), which, shot] = block.reshape(NX * NY, BX, BY)
-        core, q = lax.rem(k, 2), k // 2
-        for dx, dy in ORDER:
+                out[pl.ds(at, 16), pl.ds(64 * which + 32 * shot, BX)] = block.reshape(NX * NY, BX, BY)
+
+    def send(k, out, into, sem, q):
+        core = lax.rem(k, 2)
+        for p, (dx, dy) in enumerate(ORDER):
             tx, ty = chip(dx, dy)
-
-            def send():
-                remote(
-                    sbuf.at[k * 16 + tx * NY + ty], rbuf.at[q, me_g], asend, arecv.at[q],
-                    ty * NC + core, tx * NZ + z,
-                ).start()
-
+            copy = remote(
+                out(tx * NY + ty), into(2 * p + c), sem, arecv.at[q, p // 2],
+                ty * NC + core, tx * NZ + z,
+            )
             if (dx, dy) == (0, 0):
-                pl.when(core != c)(send)
+                pl.when(core != c)(copy.start)
             else:
-                send()
-
-        @pl.when(core == c)
-        def _():
-            rbuf[q, me_g] = sbuf[k * 16 + x * NY + y]
-
-    pltpu.make_async_copy(cland.at[pl.ds(0, GROUP - 1)], cland.at[pl.ds(0, GROUP - 1)], crecv).wait()
-
-    @pl.loop(0, GROUP // 4)
-    def _(i):
+                copy.start()
+
+    for k in range(2):
+        turn(k, head_out, 16 * k)
+        for h in range(16):
+            head_out[16 * k + h, pl.ds(128, 8)] = note
+
+        @pl.when(c == k)
+        def _():
+            head_in[me_slot, pl.ds(0, 136)] = head_out[16 * k + x * NY + y, pl.ds(0, 136)]
+
+    edges = (me_t > 0).astype(jnp.int32) + (me_t < last).astype(jnp.int32)
+    pl.semaphore_wait(barrier, GROUP - 1 + 2 * NC + NY * NC * edges)
+
+    for k in range(2):
+        send(
+            k,
+            lambda chip: head_out.at[16 * k + chip, pl.ds(0, 136)],
+            lambda slot: head_in.at[slot, pl.ds(0, 136)],
+            headsend,
+            0,
+        )
+
+    @pl.loop(2, NZ)
+    def _(k):
+        q = k // 2
+        at = (k - 2) * 16
+        turn(k, sbuf, at)
+        send(k, lambda chip: sbuf.at[at + chip], lambda slot: rbuf.at[q - 1, slot], asend, q)
+
+        @pl.when(lax.rem(k, 2) == c)
+        def _():
+            rbuf[q - 1, me_slot] = sbuf[at + x * NY + y]
+
+    def tables(i):
         row = lax.broadcasted_iota(jnp.int32, (X, 128), 0)
+        wide = lax.broadcasted_iota(jnp.int32, (BX, 128), 1)
+        first = wide[0:1]
+        notes = [head_in[4 * i + s, pl.ds(128, 8)].astype(F32)[0:1].astype(jnp.int32) for s in range(4)]
         for h in range(2):
-            one = cland[4 * i + 2 * h]
-            two = cland[4 * i + 2 * h + 1]
-            both = jnp.where(lane < 64, one, pltpu.roll(two, 64, 1))
+            both = jnp.where(first < 64, notes[2 * h], pltpu.roll(notes[2 * h + 1], 64, 1))
             rows[i, :, pl.ds(h * 128, 128)] = (row == both).astype(F32).astype(BF16)
-        wide = lax.broadcasted_iota(jnp.int32, (BX, 128), 1)
         for s in range(4):
-            msg = cland[4 * i + s]
             for shot in range(2):
-                col = msg[:, 64 + 32 * shot : 65 + 32 * shot]
+                col = notes[s][:, 64 + 32 * shot : 65 + 32 * shot]
                 left = (wide >= col).astype(F32).astype(BF16)
                 mask[i, pl.ds((2 * s + shot) * BX, BX), :] = left
 
     def place(q):
-        pltpu.make_async_copy(
-            rbuf.at[q, pl.ds(0, GROUP - 1)], rbuf.at[q, pl.ds(0, GROUP - 1)], arecv.at[q]
-        ).wait()
+        def arrive(i, count):
+            if q == 0:
+                part = head_in.at[pl.ds(0, count), pl.ds(0, 136)]
+            else:
+                part = rbuf.at[q - 1, pl.ds(0, count)]
+            pltpu.make_async_copy(part, part, arecv.at[q, i]).wait()
 
         def step(i, fresh):
-            got = rbuf[q, pl.ds(4 * i, 4)]
-            wave = got[:, 0].reshape(256, BY).astype(F32)
-            back = got[:, 1].reshape(256, BY).astype(F32)
+            if q == 0:
+                tables(i)
+            got = head_in[pl.ds(4 * i, 4)] if q == 0 else rbuf[q - 1, pl.ds(4 * i, 4)]
+            wave = got[:, 0:64].reshape(256, BY).astype(F32)
+            back = got[:, 64:128].reshape(256, BY).astype(F32)
             keep = mask[i]
             table = rows[i]
             for which, value in ((0, wave * back), (1, wave * wave)):
@@ -186,11 +205,16 @@
                 else:
                     obuf[q, which] += part
 
+        arrive(0, 4)
         step(0, True)
 
-        @pl.loop(1, GROUP // 4)
+        @pl.loop(1, BLOCKS - 1)
         def _(i):
+            arrive(i, 4)
             step(i, False)
+
+        arrive(BLOCKS - 1, 3)
+        step(BLOCKS - 1, False)
 
     def begin_up():
         return remote(obuf.at[0, 0], cbuf.at[0, 0], bsend.at[0], brecv.at[0], y * NC + 1, x * NZ + up)
@@ -199,8 +223,17 @@
         return remote(obuf.at[0, 1], cbuf.at[1, 1], bsend.at[1], brecv.at[1], y * NC, x * NZ + down)
 
     def pass_down(q):
-        slot, core = (q + 1, 0) if q < 3 else (4, 1)
-        return remote(obuf.at[q], cbuf.at[slot], bsend.at[q + 1], brecv.at[slot], y * NC + core, x * NZ + down)
+        return remote(obuf.at[q], cbuf.at[q + 1], bsend.at[q + 1], brecv.at[q + 1], y * NC, x * NZ + down)
+
+    def last_down(p):
+        part = pl.ds(64 * p, 64)
+        return tuple(
+            remote(
+                obuf.at[3, h, part], cbuf.at[4, h, part], bsend.at[4 + 2 * p + h], brecv.at[4 + 2 * p + h],
+                y * NC + 1, x * NZ + down,
+            )
+            for h in range(2)
+        )
 
     def pass_up(q):
         return remote(obuf.at[q], cbuf.at[q + 1], bsend.at[q + 1], brecv.at[q + 1], y * NC + 1, x * NZ + up)
@@ -219,8 +252,15 @@
                 pass_down(1).start()
             else:
                 pass_down(q - 1).wait_recv()
-                obuf[q] += cbuf[q]
-                pass_down(q).start()
+                if q < 3:
+                    obuf[q] += cbuf[q]
+                    pass_down(q).start()
+                else:
+                    for p in range(4):
+                        part = pl.ds(64 * p, 64)
+                        obuf[3, :, part] += cbuf[3, :, part]
+                        for copy in last_down(p):
+                            copy.start()
 
         @pl.when(c == 1)
         def _():
@@ -234,7 +274,6 @@
                 pass_up(q).start()
             else:
                 pass_up(2).wait_recv()
-                pass_down(3).wait_recv()
 
     def to_strip(w):
         return remote(
@@ -253,20 +292,22 @@
 
     @pl.when(c == 1)
     def _():
-        image = obuf[3, 0] + cbuf[3, 0] + cbuf[4, 0]
-        light = obuf[3, 1] + cbuf[3, 1] + cbuf[4, 1]
         nbuf[pl.ds(0, 8)] = jnp.zeros((8, Y), F32)
         nbuf[pl.ds(X + 8, 8)] = jnp.zeros((8, Y), F32)
-        nbuf[pl.ds(8, X)] = image / (1.0 + light)
+        for p in range(4):
+            for copy in last_down(p):
+                copy.wait_recv()
+            part = pl.ds(64 * p, 64)
+            image = obuf[3, 0, part] + cbuf[3, 0, part] + cbuf[4, 0, part]
+            light = obuf[3, 1, part] + cbuf[3, 1, part] + cbuf[4, 1, part]
+            nbuf[pl.ds(64 * p + 8, 64)] = image / (1.0 + light)
 
         @pl.loop(1, NY * NC)
         def _(k):
             to_strip(lax.rem(me_w + k, NY * NC)).start()
 
         @pl.loop(0, NY * NC)
-        def _(k):
-            w = lax.rem(me_w + k, NY * NC)
-
+        def _(w):
             @pl.when(to_later)
             def _():
                 to_side(w, 0, me_t + 1).start()
@@ -308,29 +349,29 @@
         after = jnp.where(column == Y - 1, 0.0, pltpu.roll(center, Y - 1, 1))
         out_ref[j] = beside + (before + after) - 6.0 * center
 
-    pltpu.make_async_copy(sbuf.at[pl.ds(0, 124)], sbuf.at[pl.ds(0, 124)], asend).wait()
-    pltpu.make_async_copy(cland.at[pl.ds(0, GROUP - 1)], cland.at[pl.ds(0, GROUP - 1)], csend).wait()
+    for part, sem in ((head_out.at[pl.ds(0, 31), pl.ds(0, 136)], headsend), (sbuf.at[pl.ds(0, 93)], asend)):
+        pltpu.make_async_copy(part, part, sem).wait()
 
     @pl.when(c == 0)
     def _():
         begin_up().wait_send()
         begin_down().wait_send()
-        for q in range(1, 4):
+        for q in range(1, 3):
             pass_down(q).wait_send()
+        for p in range(4):
+            for copy in last_down(p):
+                copy.wait_send()
 
     @pl.when(c == 1)
     def _():
         for q in range(3):
             pass_up(q).wait_send()
-
         @pl.loop(1, NY * NC)
         def _(k):
             to_strip(lax.rem(me_w + k, NY * NC)).wait_send()
 
         @pl.loop(0, NY * NC)
-        def _(k):
-            w = lax.rem(me_w + k, NY * NC)
-
+        def _(w):
             @pl.when(to_later)
             def _():
                 to_side(w, 0, me_t + 1).wait_send()
@@ -356,18 +397,18 @@
         scratch_shapes=[
             pltpu.SMEM((2, 2), jnp.int32),
             pltpu.VMEM((NZ, 2, 2, NX, NY, BX, BY), BF16),
-            pltpu.VMEM((NZ * NX * NY, 2, 2, BX, BY), BF16),
-            pltpu.VMEM((4, GROUP, 2, 2, BX, BY), BF16),
-            pltpu.VMEM((1, 128), jnp.int32),
-            pltpu.VMEM((GROUP, 1, 128), jnp.int32),
-            pltpu.VMEM((GROUP // 4, X, 256), BF16),
-            pltpu.VMEM((GROUP // 4, 256, 128), BF16),
+            pltpu.VMEM((2 * NX * NY, 144, BY), BF16),
+            pltpu.VMEM((6 * NX * NY, 128, BY), BF16),
+            pltpu.VMEM((GROUP, 144, BY), BF16),
+            pltpu.VMEM((3, GROUP, 128, BY), BF16),
+            pltpu.VMEM((BLOCKS, X, 256), BF16),
+            pltpu.VMEM((BLOCKS, 256, 128), BF16),
             pltpu.VMEM((4, 2, X, Y), F32),
             pltpu.VMEM((5, 2, X, Y), F32),
             pltpu.VMEM((X + 16, Y), F32),
             pltpu.VMEM((PLANES + 2, STRIP + 16, Y), F32),
-            dma, dma((NZ, 2)), dma, dma((4,)), dma, dma,
-            dma((5,)), dma((5,)), dma((8,)), dma((8,)), dma((6,)),
+            dma, dma((NZ, 2)), dma, dma, dma((4, BLOCKS)),
+            dma((12,)), dma((12,)), dma((8,)), dma((8,)), dma((6,)),
         ],
         compiler_params=pltpu.CompilerParams(
             collective_id=0, has_side_effects=True, vmem_limit_bytes=67043328

time: 73.8 us -> 72.5 us (0.982)
  the two profiles are of different devices: /device:TPU:3 before, /device:TPU:27 now
where the time goes in v3:
time: 72.5 us; the launch traced here: 71.6 us
  Pallas kernels  70 us (97%)
  local copies, waits for them, and re-layouts  1.57 us (2%)
    pallas_call x1, Pallas kernels, per_device(): pl.pallas_call(kernel, out_shape=jax.ShapeDtypeStruct((PLANES, STRIP, Y),...  70 us
    unnamed x1, local copies, waits for them, and re-layouts  1.57 us

profile of v3, /device:TPU:27, one launch (start us, length us, event | category | flops | bytes accessed | tf_op | source)
XLA Modules:
  0.0 71.6 jit_solution(16483932958201513001)
XLA Ops:
  0.0 70.0 %stack_shots.1 = f32[4,32,256]{2,1,0:T(8,128)} custom-call(s32[2,2]{1,0:T(2,128)} %corners_hbm.1, bf16[2,4,8,4,32,128]{5,4,3,2,1,0:T(8,128)(2,1)} %bitcast.2, bf16[2,4,8,4,32,128]{5,4,3,2,1,0:T(8,128)(2,1)} %bitcast.3), custom_call_target="tpu_custom_call" | custom-call | tf_op jit(solution)/shard_map/stack_shots/pallas_call | solution.py:388
  70.0 1.6 %copy.5 = f32[4,32,256]{2,1,0:T(8,128)} copy(f32[4,32,256]{2,1,0:T(8,128)} %stack_shots.1) | data formatting | bytes 262144

commit v4 on v3

--- a/solution.py
+++ b/solution.py
@@ -302,19 +302,21 @@
             light = obuf[3, 1, part] + cbuf[3, 1, part] + cbuf[4, 1, part]
             nbuf[pl.ds(64 * p + 8, 64)] = image / (1.0 + light)
 
-        @pl.loop(1, NY * NC)
-        def _(k):
-            to_strip(lax.rem(me_w + k, NY * NC)).start()
-
-        @pl.loop(0, NY * NC)
-        def _(w):
-            @pl.when(to_later)
-            def _():
-                to_side(w, 0, me_t + 1).start()
-
-            @pl.when(to_earlier)
-            def _():
-                to_side(w, 5, me_t - 1).start()
+            @pl.loop(2 * p, 2 * p + 2)
+            def _(w):
+                @pl.when(to_later)
+                def _():
+                    to_side(w, 0, me_t + 1).start()
+
+                @pl.when(to_earlier)
+                def _():
+                    to_side(w, 5, me_t - 1).start()
+
+            @pl.loop((0, 1, 3, 5)[p], (1, 3, 5, 8)[p])
+            def _(w):
+                @pl.when(w != me_w)
+                def _():
+                    to_strip(w).start()
 
         fbuf[1 + y] = nbuf[pl.ds(pl.multiple_of(me_w * STRIP, 8), STRIP + 16)]
 

time: 72.5 us -> 70.3 us (0.970)
  Pallas kernels: 70 us -> 67.8 us
    pallas_call x1, Pallas kernels: 70 us -> 67.8 us  [per_device(): pl.pallas_call(kernel, out_shape=jax.ShapeDtypeStruct((PLANES, STRIP, Y),...]
where the time goes in v4:
time: 70.3 us; the launch traced here: 69.4 us
  Pallas kernels  67.8 us (96%)
  local copies, waits for them, and re-layouts  1.57 us (2%)
    pallas_call x1, Pallas kernels, per_device(): pl.pallas_call(kernel, out_shape=jax.ShapeDtypeStruct((PLANES, STRIP, Y),...  67.8 us
    unnamed x1, local copies, waits for them, and re-layouts  1.57 us

profile of v4, /device:TPU:27, one launch (start us, length us, event | category | flops | bytes accessed | tf_op | source)
XLA Modules:
  0.0 69.4 jit_solution(1097390071562989821)
XLA Ops:
  0.0 67.8 %stack_shots.1 = f32[4,32,256]{2,1,0:T(8,128)} custom-call(s32[2,2]{1,0:T(2,128)} %corners_hbm.1, bf16[2,4,8,4,32,128]{5,4,3,2,1,0:T(8,128)(2,1)} %bitcast.2, bf16[2,4,8,4,32,128]{5,4,3,2,1,0:T(8,128)(2,1)} %bitcast.3), custom_call_target="tpu_custom_call" | custom-call | tf_op jit(solution)/shard_map/stack_shots/pallas_call | solution.py:390
  67.8 1.6 %copy.5 = f32[4,32,256]{2,1,0:T(8,128)} copy(f32[4,32,256]{2,1,0:T(8,128)} %stack_shots.1) | data formatting | bytes 262144

commit v5 on v4

--- a/solution.py
+++ b/solution.py
@@ -60,6 +60,12 @@
             pltpu.make_async_copy(rcv_hbm.at[:, :, zt], lbuf.at[k, 1], lsem.at[k, 1]),
         )
 
+    corners_copy = pltpu.make_async_copy(corners_hbm, corners_ref, cornersem)
+    corners_copy.start()
+    for k in range(2):
+        for copy in load(k):
+            copy.start()
+
     barrier = pltpu.get_barrier_semaphore()
 
     def greet(w, t):
@@ -85,10 +91,7 @@
         def _():
             greet(w, me_t + 1)
 
-    corners_copy = pltpu.make_async_copy(corners_hbm, corners_ref, cornersem)
-    corners_copy.start()
-
-    @pl.loop(0, NZ)
+    @pl.loop(2, NZ)
     def _(k):
         for copy in load(k):
             copy.start()
@@ -130,7 +133,7 @@
             else:
                 copy.start()
 
-    for k in range(2):
+    def turn_head(k):
         turn(k, head_out, 16 * k)
         for h in range(16):
             head_out[16 * k + h, pl.ds(128, 8)] = note
@@ -139,10 +142,7 @@
         def _():
             head_in[me_slot, pl.ds(0, 136)] = head_out[16 * k + x * NY + y, pl.ds(0, 136)]
 
-    edges = (me_t > 0).astype(jnp.int32) + (me_t < last).astype(jnp.int32)
-    pl.semaphore_wait(barrier, GROUP - 1 + 2 * NC + NY * NC * edges)
-
-    for k in range(2):
+    def send_head(k):
         send(
             k,
             lambda chip: head_out.at[16 * k + chip, pl.ds(0, 136)],
@@ -150,6 +150,13 @@
             headsend,
             0,
         )
+
+    turn_head(0)
+    edges = (me_t > 0).astype(jnp.int32) + (me_t < last).astype(jnp.int32)
+    pl.semaphore_wait(barrier, GROUP - 1 + 2 * NC + NY * NC * edges)
+    send_head(0)
+    turn_head(1)
+    send_head(1)
 
     @pl.loop(2, NZ)
     def _(k):
@@ -413,7 +420,7 @@
             dma((12,)), dma((12,)), dma((8,)), dma((8,)), dma((6,)),
         ],
         compiler_params=pltpu.CompilerParams(
-            collective_id=0, has_side_effects=True, vmem_limit_bytes=67043328
+            collective_id=0, has_side_effects=True, vmem_limit_bytes=56000000
         ),
         name="stack_shots",
     )(corners, source, receiver)

time: 70.3 us -> 69.4 us (0.987)
  Pallas kernels: 67.8 us -> 67 us
    pallas_call x1, Pallas kernels: 67.8 us -> 67 us  [per_device(): pl.pallas_call(kernel, out_shape=jax.ShapeDtypeStruct((PLANES, STRIP, Y),...]
    unnamed x1 -> x3, local copies, waits for them, and re-layouts: 1.57 us -> 1.34 us
where the time goes in v5:
time: 69.4 us; the launch traced here: 68.4 us
  Pallas kernels  67 us (97%)
  local copies, waits for them, and re-layouts  1.34 us (2%)
    pallas_call x1, Pallas kernels, per_device(): pl.pallas_call(kernel, out_shape=jax.ShapeDtypeStruct((PLANES, STRIP, Y),...  67 us

profile of v5, /device:TPU:27, one launch (start us, length us, event | category | flops | bytes accessed | tf_op | source)
XLA Modules:
  0.0 68.4 jit_solution(8849170668086580221)
XLA Ops:
  0.0 0.0 copy-start
  0.0 0.7 copy-done
  0.7 67.0 %stack_shots.1 = f32[4,32,256]{2,1,0:T(8,128)S(1)} custom-call(s32[2,2]{1,0:T(2,128)S(1)} %copy-done, bf16[2,4,8,4,32,128]{5,4,3,2,1,0:T(8,128)(2,1)} %bitcast.2, bf16[2,4,8,4,32,128]{5,4,3,2,1,0:T(8,128)(2,1)} %bitcast.3), custom_call_target="tpu_custom_call" | custom-call | tf_op jit(solution)/shard_map/stack_shots/pallas_call | solution.py:397
  67.7 0.7 copy.5
Async XLA Ops:
  0.0 0.7 copy-start

commit v6 on v5

--- a/solution.py
+++ b/solution.py
@@ -21,8 +21,8 @@
 BF16 = jnp.bfloat16
 
 ORDER = (
-    (1, 0), (0, 1), (3, 3), (2, 1), (0, 3), (1, 2), (3, 0), (2, 2),
-    (1, 1), (0, 2), (3, 1), (2, 3), (1, 3), (3, 2), (2, 0), (0, 0),
+    (0, 3), (3, 0), (0, 1), (1, 0), (0, 2), (1, 3), (2, 0), (3, 1),
+    (1, 1), (3, 3), (2, 1), (2, 3), (1, 2), (3, 2), (2, 2), (0, 0),
 )
 
 
@@ -420,7 +420,7 @@
             dma((12,)), dma((12,)), dma((8,)), dma((8,)), dma((6,)),
         ],
         compiler_params=pltpu.CompilerParams(
-            collective_id=0, has_side_effects=True, vmem_limit_bytes=56000000
+            collective_id=0, has_side_effects=True, vmem_limit_bytes=56_000_000
         ),
         name="stack_shots",
     )(corners, source, receiver)

time: 69.4 us -> 68.9 us (level); the launches traced: 68.4 us -> 68.8 us
  no operation moved by 1% of the time
where the time goes in v6:
time: 68.9 us; the launch traced here: 68.8 us
  Pallas kernels  67.5 us (98%)
  local copies, waits for them, and re-layouts  1.34 us (2%)
    pallas_call x1, Pallas kernels, per_device(): pl.pallas_call(kernel, out_shape=jax.ShapeDtypeStruct((PLANES, STRIP, Y),...  67.5 us

profile of v6, /device:TPU:27, one launch (start us, length us, event | category | flops | bytes accessed | tf_op | source)
XLA Modules:
  0.0 68.8 jit_solution(5781894403223800655)
XLA Ops:
  0.0 0.0 copy-start
  0.0 0.7 copy-done
  0.7 67.5 %stack_shots.1 = f32[4,32,256]{2,1,0:T(8,128)S(1)} custom-call(s32[2,2]{1,0:T(2,128)S(1)} %copy-done, bf16[2,4,8,4,32,128]{5,4,3,2,1,0:T(8,128)(2,1)} %bitcast.2, bf16[2,4,8,4,32,128]{5,4,3,2,1,0:T(8,128)(2,1)} %bitcast.3), custom_call_target="tpu_custom_call" | custom-call | tf_op jit(solution)/shard_map/stack_shots/pallas_call | solution.py:397
  68.1 0.7 copy.5
Async XLA Ops:
  0.0 0.7 copy-start

commit v7 on v6

--- a/solution.py
+++ b/solution.py
@@ -71,10 +71,11 @@
     def greet(w, t):
         pl.semaphore_signal(barrier, inc=1, device_id=(w, t), device_id_type=MESH)
 
-    @pl.loop(1, GROUP)
-    def _(g):
-        other = lax.rem(me_g + g, GROUP)
-        greet(lax.rem(other, NY * NC), (other // (NY * NC)) * NZ + z)
+    for dx, dy in ORDER[:-1]:
+        tx, ty = chip(dx, dy)
+        for k in range(NC):
+            greet(ty * NC + k, tx * NZ + z)
+    greet(y * NC + 1 - c, me_t)
 
     for k in range(NC):
         greet(y * NC + k, x * NZ + up)

time: 68.9 us -> 68.6 us (level)
  no operation moved by 1% of the time
where the time goes in v7:
time: 68.6 us; the launch traced here: 68.5 us
  Pallas kernels  67.2 us (98%)
  local copies, waits for them, and re-layouts  1.34 us (2%)
    pallas_call x1, Pallas kernels, per_device(): pl.pallas_call(kernel, out_shape=jax.ShapeDtypeStruct((PLANES, STRIP, Y),...  67.2 us

profile of v7, /device:TPU:27, one launch (start us, length us, event | category | flops | bytes accessed | tf_op | source)
XLA Modules:
  0.0 68.5 jit_solution(2298616218464641822)
XLA Ops:
  0.0 0.0 copy-start
  0.0 0.7 copy-done
  0.7 67.2 %stack_shots.1 = f32[4,32,256]{2,1,0:T(8,128)S(1)} custom-call(s32[2,2]{1,0:T(2,128)S(1)} %copy-done, bf16[2,4,8,4,32,128]{5,4,3,2,1,0:T(8,128)(2,1)} %bitcast.2, bf16[2,4,8,4,32,128]{5,4,3,2,1,0:T(8,128)(2,1)} %bitcast.3), custom_call_target="tpu_custom_call" | custom-call | tf_op jit(solution)/shard_map/stack_shots/pallas_call | solution.py:398
  67.9 0.7 copy.5
Async XLA Ops:
  0.0 0.7 copy-start
